TPU v7x, 32 devices: a whole 2x2x4 slice. The times are simulated.
32 devices in a mesh: prow: 4 (over y, x), pcol: 8 (over z, core).
Axes of the slice: x: 2, y: 2, z: 4, core: 2. Of those that a mesh axis runs over, the one named last changes fastest.
Arguments:
- panel_t: float32 [8, 256, 4096], P('pcol', None, 'prow'), may hold values from -0.09375 to 0.09375
- ancestor: float32 [4096, 4096], P('prow', 'pcol'), as said below
- structure: int32 [8, 16], replicated, may hold values 0 or 1
- diag_inv: float32 [8, 256, 256], P('pcol'), may hold values from -6 to 6
Outputs:
- inverse_panel: float32 [2048, 4096], P('pcol', 'prow')
- inverse_diag: float32 [8, 256, 256], P('pcol')
Inputs may be any that keep to these rules, and one draw needn't show every extreme that they name: ancestor is symmetric up to rounding.
All inputs are finite; a program needn't handle non-finite values.
Results may differ from a plain program's by a relative error of at most 0.00007.
Values sent between devices are 32-bit elements; how exact they have to be, the bound alone decides.
A program may use at most 128 MiB of HBM per device.

v0:
```python
import jax
import jax.numpy as jnp
from jax import lax
from jax.sharding import PartitionSpec as P


def local(panel_t, ancestor, structure, diag_inv):
    local_sn = panel_t.shape[0]
    width = panel_t.shape[1]
    row_span = panel_t.shape[2]
    row_blocks = row_span // width
    col_index = lax.axis_index("pcol")
    row_index = lax.axis_index("prow")
    mine = lax.dynamic_slice(
        structure, (col_index * local_sn, row_index * row_blocks), (local_sn, row_blocks)
    )
    masked = (
        panel_t.reshape(local_sn, width, row_blocks, width)
        * mine.astype(jnp.float32)[:, None, :, None]
    )
    masked = masked.reshape(local_sn, width, row_span)
    prow_size = lax.axis_size("prow")
    rows_here = width // prow_size
    arranged = masked.reshape(local_sn, prow_size, rows_here, row_span).transpose(1, 0, 2, 3)
    gathered = lax.all_gather(arranged, "pcol", axis=1, tiled=True)
    total_nodes = gathered.shape[1]
    flat_rows = gathered.reshape(prow_size * total_nodes * rows_here, row_span)
    reduced = lax.psum_scatter(
        jnp.dot(
            flat_rows, ancestor, precision=lax.Precision.HIGHEST, preferred_element_type=jnp.float32
        ),
        "prow",
        scatter_dimension=0,
        tiled=True,
    )
    moved = lax.all_to_all(
        lax.all_to_all(reduced, "pcol", split_axis=0, concat_axis=1, tiled=True),
        "prow",
        split_axis=1,
        concat_axis=0,
        tiled=True,
    )
    summed = moved.reshape(prow_size, local_sn, rows_here, row_span).transpose(1, 0, 2, 3)
    summed = summed.reshape(local_sn * width, row_span)
    inverse_panel = -summed
    blocks = inverse_panel.reshape(local_sn, width, row_span)
    partial_diag = jnp.einsum("kbj,kcj->kbc", blocks, masked, precision=lax.Precision.HIGHEST)
    inverse_diag = diag_inv - lax.psum(partial_diag, "prow")
    return (inverse_panel, inverse_diag)


def solution(mesh):
    return jax.shard_map(
        local,
        mesh=mesh,
        in_specs=(P("pcol", None, "prow"), P("prow", "pcol"), P(), P("pcol", None, None)),
        out_specs=(P("pcol", "prow"), P("pcol", None, None)),
        check_vma=False,
    )
```

profile of v0, /device:TPU:24, one launch (start us, length us, event | category | flops | bytes accessed | tf_op | source)
XLA Modules:
  0.0 268.1 jit_solution(682398275534982507)
XLA Ops:
  7.2 0.0 copy-start
  7.2 0.0 all-gather.2.cloned.1.call-start
  7.2 0.9 convert_bitcast_fusion
  8.1 0.1 broadcast_bitcast_fusion
  8.2 2.3 broadcast_multiply_fusion
  10.5 0.0 all-gather.2.cloned.1.call-update
  10.5 0.0 reduce-scatter.2.cloned.1.call-start
  10.6 80.4 %all-gather.2.cloned.1.call-done = f32[4,8,64,1024]{3,2,1,0:T(8,128)} async-done(((f32[4,1,64,1024]{3,2,1,0:T(8,128)}), f32[4,8,64,1024]{3,2,1,0:T(8,128)}) %all-gather.2.cloned.1.call-update) | async-done | bytes 8388624 | tf_op jit(solution)/shard_map/all_gather | solution.py:25
  91.0 0.0 copy-done
  91.0 16.9 %fusion.3 = f32[2048,512]{1,0:T(8,128)} fusion(f32[2048,1024]{1,0:T(8,128)} %bitcast.27, f32[1024,512]{1,0:T(8,128)S(1)} %copy-done), kind=kOutput, calls=%fused_computation.7 | convolution fusion | flops 12884901888 | bytes 14680064 | tf_op jit(solution)/shard_map/dot_general | solution.py:29
  107.8 0.0 reduce-scatter.2.cloned.1.call-update
  107.9 0.0 all-reduce.2.cloned.1.call-start
  107.9 53.9 %reduce-scatter.2.cloned.1.call-done = f32[512,512]{1,0:T(8,128)} async-done(((f32[2048,512]{1,0:T(8,128)}), f32[512,512]{1,0:T(8,128)}) %reduce-scatter.2.cloned.1.call-update) | async-done | bytes 1048592 | tf_op jit(solution)/shard_map/reduce_scatter | solution.py:28
  161.9 29.1 %all_to_all.29 = f32[8,64,512]{2,1,0:T(8,128)S(1)} all-to-all(f32[8,64,512]{2,1,0:T(8,128)} %bitcast.24), channel_id=1, replica_groups=mesh['prow'=4,'pcol'=8] {'pcol'}, dimensions={0} | all-to-all | bytes 2097152 | tf_op jit(solution)/shard_map/all_to_all | solution.py:37
  191.0 1.6 copy.9
  192.6 0.0 copy-start.1
  192.6 2.8 %all_to_all.25 = f32[64,4,1024]{2,1,0:T(4,128)} reshape(f32[64,8,512]{2,1,0:T(8,128)} %copy.9) | data formatting | bytes 2097152 | tf_op jit(solution)/shard_map/all_to_all | solution.py:36
  195.4 0.0 copy-start.3
  195.4 1.9 copy.10
  197.2 17.1 %all_to_all.30 = f32[64,4,1024]{2,0,1:T(8,128)S(1)} all-to-all(f32[64,4,1024]{2,0,1:T(8,128)S(1)} %copy.10), channel_id=1, replica_groups=mesh['prow'=4,'pcol'=8] {'prow'}, dimensions={1} | all-to-all | bytes 2097152 | tf_op jit(solution)/shard_map/all_to_all | solution.py:36
  214.3 0.1 neg.13
  214.4 0.0 copy-start.2
  214.4 1.0 copy-done.2
  215.4 0.0 copy-done.1
  215.4 1.8 convolution_bitcast_fusion
  217.2 0.0 all-reduce.2.cloned.1.call-update
  217.2 42.6 %all-reduce.2.cloned.1.call-done = f32[1,256,256]{2,1,0:T(8,128)} async-done(((f32[1,256,256]{2,1,0:T(8,128)}), f32[1,256,256]{2,1,0:T(8,128)}) %all-reduce.2.cloned.1.call-update) | async-done | bytes 262160 | tf_op jit(solution)/shard_map/psum | solution.py:48
  259.8 0.0 copy-done.3
  259.8 1.7 sub.3
  (1 shorter events, 0.0 us)
Async XLA Ops:
  7.2 83.8 %copy-start = (f32[1024,512]{1,0:T(8,128)S(1)}, f32[1024,512]{1,0:T(8,128)}, u32[]{:S(2)}) copy-start(f32[1024,512]{1,0:T(8,128)} %param.5) | copy-start | bytes 6291460
  7.2 83.8 %all-gather.2.cloned.1.call-start = ((), (), s32[]{:S(2)}) async-start(), calls=%async_computation.3 | async-start | bytes 9437184 | tf_op jit(solution)/shard_map/all_gather | solution.py:25
  10.5 151.3 %reduce-scatter.2.cloned.1.call-start = ((), (), s32[]{:S(2)}) async-start(), calls=%async_computation.4 | async-start | bytes 5242880 | tf_op jit(solution)/shard_map/reduce_scatter | solution.py:28
  107.9 151.9 %all-reduce.2.cloned.1.call-start = ((), (), s32[]{:S(2)}) async-start(), calls=%async_computation.5 | async-start | bytes 524288 | tf_op jit(solution)/shard_map/psum | solution.py:48
  192.6 22.8 %copy-start.1 = (f32[1,256,1024]{2,1,0:T(8,128)S(1)}, f32[1,256,1024]{2,1,0:T(8,128)}, u32[]{:S(2)}) copy-start(f32[1,256,1024]{2,1,0:T(8,128)} %param.4) | copy-start | bytes 3145732
  195.4 64.5 %copy-start.3 = (f32[1,256,256]{2,1,0:T(8,128)S(1)}, f32[1,256,256]{2,1,0:T(8,128)}, u32[]{:S(2)}) copy-start(f32[1,256,256]{2,1,0:T(8,128)} %param.7) | copy-start | bytes 786436
  214.4 1.0 copy-start.2
Sparse Core Ops, SparseCore 0:
  10.7 80.2 all-gather.1
  108.0 53.8 reduce-scatter.1
  217.3 42.4 all-reduce.1
where the time goes:
time: 270 us; the launch traced here: 268 us
  waiting for transfers between devices  177 us (66%)
  blocking collectives  46.2 us (17%)
  matrix products  18.6 us (7%)
  between operations  13.8 us (5%)
  local copies, waits for them, and re-layouts  7.31 us (3%)
  other arithmetic  5.02 us (2%)
    all_gather x1, waiting for transfers between devices, local(): gathered = lax.all_gather(arranged, 'pcol', axis=1, tiled=True)  80.4 us
    reduce_scatter x1, waiting for transfers between devices, local(): lax.psum_scatter(jnp.dot(flat_rows, ancestor, precision=lax.Precision.HIG...  53.9 us
    psum x1, waiting for transfers between devices, local(): inverse_diag = diag_inv - lax.psum(partial_diag, 'prow')  42.6 us
    all_to_all x1, blocking collectives, local(): lax.all_to_all(reduced, 'pcol', split_axis=0, concat_axis=1, tiled=True)  29.1 us
    all_to_all x1, blocking collectives, local(): lax.all_to_all(lax.all_to_all(reduced, 'pcol', split_axis=0, concat_axis=...  17.1 us
    dot_general x1, matrix products, local(): jnp.dot(flat_rows, ancestor, precision=lax.Precision.HIGHEST, preferred_e...  16.9 us
  transfers between devices with their start and end apart: 3, of which 3 were waited for; matrix products, arithmetic and copies ran while one was open for 0% of the time, Pallas kernels for 0%

commit v1 on v0

v1 whole, which is shorter than its diff:
```python
import functools

import jax
import jax.numpy as jnp
from jax import lax
from jax.experimental import pallas as pl
from jax.experimental.pallas import tpu as pltpu
from jax.sharding import PartitionSpec as P

MESH = pl.DeviceIdType.MESH
f32 = jnp.float32
bf16 = jnp.bfloat16


def split(x):
    hi = x.astype(bf16)
    return hi, (x - hi.astype(f32)).astype(bf16)


def product(x, w_hi, w_lo, dims):
    hi, lo = split(x)
    rows = x.shape[0]
    both = lax.dot_general(
        jnp.concatenate([hi, lo], axis=0), w_hi, dims, preferred_element_type=f32
    )
    return both[:rows] + (
        both[rows:] + lax.dot_general(hi, w_lo, dims, preferred_element_type=f32)
    )


def kernel(
    n, nz, g,
    st_ref, panel_ref, anc_ref, diag_ref, inv_ref, out_diag_ref,
    gath, part, rs, sums, fin, a_recv, a_hi, a_lo, m_hi, m_lo, dpart, drecv, dsum, dout,
    a_send_sem, a_recv_sem, right_sem, left_sem, gath_sem, part_sem, rs_sem,
    sum_sem, fin_sem, dp_sem, dr_sem, db_sem, do_sem,
):
    r = lax.axis_index("prow")
    me = lax.axis_index("pcol")
    z, c = me // g, me % g
    width = panel_ref.shape[1]
    ch = width // n
    nb = panel_ref.shape[2] // width
    cols = anc_ref.shape[1]

    def dev(row, plane):
        return (row, plane * g + c)

    def copy(src, dst, s, d, to):
        return pltpu.make_async_remote_copy(
            src_ref=src, dst_ref=dst, send_sem=s, recv_sem=d, device_id=to, device_id_type=MESH
        )

    barrier = pltpu.get_barrier_semaphore()
    for step in range(1, n * nz):
        other = lax.rem(r * nz + z + step, n * nz)
        pl.semaphore_signal(barrier, inc=1, device_id=dev(other // nz, other % nz), device_id_type=MESH)
    for o in range(1, g):
        pl.semaphore_signal(
            barrier, inc=1, device_id=(r, z * g + lax.rem(c + o, g)), device_id_type=MESH
        )

    mask = [st_ref[me, r * nb + j].astype(f32) for j in range(nb)]
    for q in range(n):
        for j in range(nb):
            at = slice(j * width, (j + 1) * width)
            gath[z, q, :, at] = panel_ref[0, q * ch : (q + 1) * ch, at] * mask[j]

    pl.semaphore_wait(barrier, n * nz - 1 + g - 1)

    def a_copy(o):
        return copy(
            anc_ref, a_recv.at[o - 1], a_send_sem.at[o - 1], a_recv_sem.at[o - 1],
            (r, z * g + lax.rem(c + o, g)),
        )

    for o in range(1, g):
        a_copy(o).start()

    def to_right(b, q):
        return copy(gath.at[b, q], gath.at[b, q], right_sem.at[b, q], gath_sem.at[b, q], dev(r, z + 1))

    def to_left(b, q):
        return copy(gath.at[b, q], gath.at[b, q], left_sem.at[b, q], gath_sem.at[b, q], dev(r, z - 1))

    def part_copy(b, q):
        return copy(part.at[b, q], rs.at[b, r], part_sem.at[b, q], rs_sem.at[b, r], dev(q, z))

    def sum_copy(b):
        return copy(sums.at[b], fin.at[r], sum_sem.at[b], fin_sem.at[r], dev(z, b))

    for q in range(n):
        @pl.when(z < nz - 1)
        def _():
            to_right(z, q).start()

        @pl.when(z > 0)
        def _():
            to_left(z, q).start()

    hi, lo = split(anc_ref[...])
    a_hi[c] = hi
    a_lo[c] = lo
    for q in range(n):
        hi, lo = split(gath[z, q])
        m_hi[q * ch : (q + 1) * ch, :] = hi
        m_lo[q * ch : (q + 1) * ch, :] = lo
    for o in range(1, g):
        a_copy(o).wait_recv()
        hi, lo = split(a_recv[o - 1])
        from_core = lax.rem(c + g - o, g)
        a_hi[from_core] = hi
        a_lo[from_core] = lo

    plain = (((1,), (0,)), ((), ()))

    def process(b, q):
        x = gath[b, q]
        for h in range(g):
            p = product(x, a_hi[h], a_lo[h], plain)
            part[b, q, :, h * cols : (h + 1) * cols] = p

        @pl.when(q == r)
        def _():
            rs[b, r] = part[b, q]

        @pl.when(q != r)
        def _():
            part_copy(b, q).start()

    def add_up(b):
        for o in range(1, n):
            src = lax.rem(r + o, n)
            copy(
                part.at[b, 0], rs.at[b, src], part_sem.at[b, 0], rs_sem.at[b, src], dev(src, z)
            ).wait_recv()
        total = rs[b, 0]
        for s in range(1, n):
            total = total + rs[b, s]
        sums[b] = total
        home = (z == r) & (b == z)

        @pl.when(home)
        def _():
            fin[r] = sums[b]

        @pl.when(jnp.logical_not(home))
        def _():
            sum_copy(b).start()

    @pl.loop(0, n)
    def _(q):
        process(z, q)

    def add_step(d):
        @pl.when(z - d >= 0)
        def _():
            add_up(z - d)

        @pl.when((z + d < nz) & (d > 0))
        def _():
            add_up(z + d)

    @pl.loop(1, nz)
    def _(d):
        @pl.loop(0, n)
        def _(q):
            @pl.when(z - d >= 0)
            def _():
                to_right(z - d, q).wait_recv()

                @pl.when(z < nz - 1)
                def _():
                    to_right(z - d, q).start()

                process(z - d, q)

            @pl.when(z + d < nz)
            def _():
                to_left(z + d, q).wait_recv()

                @pl.when(z > 0)
                def _():
                    to_left(z + d, q).start()

                process(z + d, q)

        add_step(d - 1)

    add_step(nz - 1)

    trans = (((1,), (1,)), ((), ()))

    def dpart_copy(q):
        return copy(dpart.at[q], drecv.at[r], dp_sem.at[q], dr_sem.at[r], dev(q, z))

    @pl.loop(0, n)
    def _(q):
        @pl.when(jnp.logical_not((z == r) & (q == r)))
        def _():
            copy(sums.at[0], fin.at[q], sum_sem.at[0], fin_sem.at[q], dev(q, r)).wait_recv()

        x = -fin[q]
        inv_ref[pl.ds(pl.multiple_of(q * ch, ch), ch), :] = x
        dpart[q] = product(x, m_hi[...], m_lo[...], trans)

        @pl.when(q == r)
        def _():
            drecv[r] = dpart[q]

        @pl.when(q != r)
        def _():
            dpart_copy(q).start()

    for o in range(1, n):
        src = lax.rem(r + o, n)
        copy(dpart.at[0], drecv.at[src], dp_sem.at[0], dr_sem.at[src], dev(src, z)).wait_recv()
    total = drecv[0]
    for s in range(1, n):
        total = total + drecv[s]
    dsum[...] = diag_ref[0, pl.ds(pl.multiple_of(r * ch, ch), ch), :] - total

    def out_copy(o):
        return copy(dsum, dout.at[r], db_sem.at[o - 1], do_sem.at[r], dev(lax.rem(r + o, n), z))

    for o in range(1, n):
        out_copy(o).start()
    out_diag_ref[0, pl.ds(pl.multiple_of(r * ch, ch), ch), :] = dsum[...]

    for o in range(1, g):
        a_copy(o).wait_send()

    @pl.loop(0, nz)
    def _(b):
        @pl.loop(0, n)
        def _(q):
            @pl.when((z < nz - 1) & (b <= z))
            def _():
                to_right(b, q).wait_send()

            @pl.when((z > 0) & (b >= z))
            def _():
                to_left(b, q).wait_send()

            @pl.when(q != r)
            def _():
                part_copy(b, q).wait_send()

        @pl.when(jnp.logical_not((z == r) & (b == z)))
        def _():
            sum_copy(b).wait_send()

    @pl.loop(0, n)
    def _(q):
        @pl.when(q != r)
        def _():
            dpart_copy(q).wait_send()

    for o in range(1, n):
        out_copy(o).wait_send()
    for o in range(1, n):
        src = lax.rem(r + o, n)
        copy(dsum, dout.at[src], db_sem.at[0], do_sem.at[src], dev(src, z)).wait_recv()
        out_diag_ref[0, pl.ds(pl.multiple_of(src * ch, ch), ch), :] = dout[src]


def local(n, npc, panel_t, ancestor, structure, diag_inv):
    _, width, span = panel_t.shape
    cols = ancestor.shape[1]
    g = span // cols
    nz = npc // g
    ch = width // n
    dma = pltpu.SemaphoreType.DMA
    vmem = pl.BlockSpec(memory_space=pltpu.VMEM)
    return pl.pallas_call(
        functools.partial(kernel, n, nz, g),
        out_shape=(
            jax.ShapeDtypeStruct((width, span), f32),
            jax.ShapeDtypeStruct(diag_inv.shape, f32),
        ),
        in_specs=[pl.BlockSpec(memory_space=pltpu.SMEM), vmem, vmem, vmem],
        out_specs=(vmem, vmem),
        scratch_shapes=[
            pltpu.VMEM((nz, n, ch, span), f32),
            pltpu.VMEM((nz, n, ch, span), f32),
            pltpu.VMEM((nz, n, ch, span), f32),
            pltpu.VMEM((nz, ch, span), f32),
            pltpu.VMEM((n, ch, span), f32),
            pltpu.VMEM((g - 1, span, cols), f32),
            pltpu.VMEM((g, span, cols), bf16),
            pltpu.VMEM((g, span, cols), bf16),
            pltpu.VMEM((width, span), bf16),
            pltpu.VMEM((width, span), bf16),
            pltpu.VMEM((n, ch, width), f32),
            pltpu.VMEM((n, ch, width), f32),
            pltpu.VMEM((ch, width), f32),
            pltpu.VMEM((n, ch, width), f32),
            dma((g - 1,)), dma((g - 1,)),
            dma((nz, n)), dma((nz, n)), dma((nz, n)), dma((nz, n)), dma((nz, n)),
            dma((nz,)), dma((n,)),
            dma((n,)), dma((n,)), dma((n - 1,)), dma((n,)),
        ],
        compiler_params=pltpu.CompilerParams(
            collective_id=0, has_side_effects=True, vmem_limit_bytes=60 * 1024 * 1024
        ),
    )(structure, panel_t, ancestor, diag_inv)


def solution(mesh):
    return jax.shard_map(
        functools.partial(local, mesh.shape["prow"], mesh.shape["pcol"]),
        mesh=mesh,
        in_specs=(P("pcol", None, "prow"), P("prow", "pcol"), P(), P("pcol", None, None)),
        out_specs=(P("pcol", "prow"), P("pcol", None, None)),
        check_vma=False,
    )
```

time: 270 us -> 127 us (0.47)
  waiting for transfers between devices: 177 us -> 0 us
  Pallas kernels: 0 us -> 123 us
  blocking collectives: 46.2 us -> 0 us
  matrix products: 18.6 us -> 0 us
  between operations: 13.8 us -> 0.65 us
  other arithmetic: 5.02 us -> 0 us
  local copies, waits for them, and re-layouts: 7.31 us -> 3.06 us
    pallas_call x0 -> x1, Pallas kernels: none -> 123 us  [local(): pl.pallas_call(functools.partial(kernel, n, nz, g), out_shape=(jax.ShapeD...]
    all_gather x1 -> x0, waiting for transfers between devices: 80.4 us -> none  [local(): gathered = lax.all_gather(arranged, 'pcol', axis=1, tiled=True)]
    reduce_scatter x1 -> x0, waiting for transfers between devices: 53.9 us -> none  [local(): lax.psum_scatter(jnp.dot(flat_rows, ancestor, precision=lax.Precision.HIG...]
    all_to_all x2 -> x0, blocking collectives: 46.2 us -> none  [the longest x1 29.1 us: local(): lax.all_to_all(reduced, 'pcol', split_axis=0, concat_axis=1, tiled=True)]
    psum x1 -> x0, waiting for transfers between devices: 42.6 us -> none  [local(): inverse_diag = diag_inv - lax.psum(partial_diag, 'prow')]
    dot_general x2 -> x0, matrix products: 18.6 us -> none  [the longest x1 16.9 us: local(): jnp.dot(flat_rows, ancestor, precision=lax.Precision.HIGHEST, preferred_e...]
    all_to_all x3 -> x0, local copies, waits for them, and re-layouts: 6.25 us -> none  [the longest x2 4.67 us: local(): lax.all_to_all(lax.all_to_all(reduced, 'pcol', split_axis=0, concat_axis=...]
    mul x2 -> x0, other arithmetic: 3.21 us -> none  [local(): panel_t.reshape(local_sn, width, row_blocks, width)]
  transfers between devices with their start and end apart: 3 -> 0, of which waited for: 3 -> 0; matrix products, arithmetic and copies ran while one was open for 0% -> 0% of each run, Pallas kernels for 0% -> 0%
where the time goes in v1:
time: 127 us; the launch traced here: 126 us
  Pallas kernels  123 us (97%)
  local copies, waits for them, and re-layouts  3.06 us (2%)
    pallas_call x1, Pallas kernels, local(): pl.pallas_call(functools.partial(kernel, n, nz, g), out_shape=(jax.ShapeD...  123 us
    unnamed x4, local copies, waits for them, and re-layouts  3.06 us

profile of v1, /device:TPU:24, one launch (start us, length us, event | category | flops | bytes accessed | tf_op | source)
XLA Modules:
  0.0 126.4 jit_solution(15978710374422563270)
XLA Ops:
  0.6 122.7 %shard_map.59 = (f32[256,1024]{1,0:T(8,128)}, f32[1,256,256]{2,1,0:T(8,128)}) custom-call(s32[8,16]{1,0:T(8,128)} %st_ref.1, f32[1,256,1024]{2,1,0:T(8,128)} %panel_ref.1, f32[1024,512]{1,0:T(8,128)} %anc_ref.1, f32[1,256,256]{2,1,0:T(8,128)} %diag_ref.1), custom_call_target="tpu_custom_call" | custom-call | tf_op jit(solution)/shard_map/pallas_call | solution.py:275
  123.3 0.0 copy-start
  123.3 2.3 %copy.8 = f32[256,1024]{1,0:T(8,128)} copy(f32[256,1024]{1,0:T(8,128)} %get-tuple-element.4) | data formatting | bytes 2097152
  125.7 0.0 copy-done
  125.7 0.7 copy.9
Async XLA Ops:
  123.3 2.4 %copy-start = (f32[1,256,256]{2,1,0:T(8,128)S(1)}, f32[1,256,256]{2,1,0:T(8,128)}, u32[]{:S(2)}) copy-start(f32[1,256,256]{2,1,0:T(8,128)} %get-tuple-element.5) | copy-start | bytes 786436

commit v2 on v1

--- a/solution.py
+++ b/solution.py
@@ -32,8 +32,10 @@
     n, nz, g,
     st_ref, panel_ref, anc_ref, diag_ref, inv_ref, out_diag_ref,
     gath, part, rs, sums, fin, a_recv, a_hi, a_lo, m_hi, m_lo, dpart, drecv, dsum, dout,
+    pz, ext, rel,
     a_send_sem, a_recv_sem, right_sem, left_sem, gath_sem, part_sem, rs_sem,
     sum_sem, fin_sem, dp_sem, dr_sem, db_sem, do_sem,
+    scat_sem, fwd_sem, pz_sem, rel_sem, out_sem,
 ):
     r = lax.axis_index("prow")
     me = lax.axis_index("pcol")
@@ -89,14 +91,47 @@
     def sum_copy(b):
         return copy(sums.at[b], fin.at[r], sum_sem.at[b], fin_sem.at[r], dev(z, b))
 
+    def detour(b):
+        return copy(sums.at[b], rel.at[b], sum_sem.at[b], rel_sem.at[b], dev(z, z))
+
+    def detour_out(b):
+        return copy(rel.at[b], fin.at[b], out_sem.at[b], fin_sem.at[b], dev(z, b))
+
+    def scatter(q):
+        return copy(gath.at[z, q], pz.at[q], scat_sem.at[q], pz_sem.at[q], dev(q, z))
+
+    def spread(to):
+        return copy(pz.at[r], pz.at[r], fwd_sem.at[to], pz_sem.at[r], dev(to, z))
+
+    def spread_all(act):
+        for to in range(n):
+            @pl.when((r != to) & (z != to))
+            def _():
+                act(spread(to))
+
     for q in range(n):
-        @pl.when(z < nz - 1)
+        @pl.when((z < nz - 1) & (z != r))
         def _():
             to_right(z, q).start()
 
-        @pl.when(z > 0)
+        @pl.when((z > 0) & (z != r))
         def _():
             to_left(z, q).start()
+
+        @pl.when((z == r) & (z != q))
+        def _():
+            scatter(q).start()
+
+    @pl.when(z == r)
+    def _():
+        pz[r] = gath[z, r]
+        spread_all(lambda d: d.start())
+
+    @pl.loop(0, nz)
+    def _(b):
+        @pl.when(b != z)
+        def _():
+            rs[b, b] = jnp.zeros(rs.shape[2:], f32)
 
     hi, lo = split(anc_ref[...])
     a_hi[c] = hi
@@ -131,9 +166,13 @@
     def add_up(b):
         for o in range(1, n):
             src = lax.rem(r + o, n)
-            copy(
-                part.at[b, 0], rs.at[b, src], part_sem.at[b, 0], rs_sem.at[b, src], dev(src, z)
-            ).wait_recv()
+
+            @pl.when((src != b) | (b == z))
+            def _():
+                copy(
+                    part.at[b, 0], rs.at[b, src], part_sem.at[b, 0], rs_sem.at[b, src], dev(src, z)
+                ).wait_recv()
+
         total = rs[b, 0]
         for s in range(1, n):
             total = total + rs[b, s]
@@ -144,9 +183,17 @@
         def _():
             fin[r] = sums[b]
 
-        @pl.when(jnp.logical_not(home))
+        @pl.when((b != z) & (b == r))
+        def _():
+            detour(b).start()
+
+        @pl.when(jnp.logical_not(home) & ((b == z) | (b != r)))
         def _():
             sum_copy(b).start()
+
+    def pass_on(b):
+        detour(b).wait_recv()
+        detour_out(b).start()
 
     @pl.loop(0, n)
     def _(q):
@@ -160,12 +207,21 @@
         @pl.when((z + d < nz) & (d > 0))
         def _():
             add_up(z + d)
+
+    def pass_step(d):
+        @pl.when((z == r) & (z - d >= 0) & (d > 0))
+        def _():
+            pass_on(z - d)
+
+        @pl.when((z == r) & (z + d < nz) & (d > 0))
+        def _():
+            pass_on(z + d)
 
     @pl.loop(1, nz)
     def _(d):
         @pl.loop(0, n)
         def _(q):
-            @pl.when(z - d >= 0)
+            @pl.when((z - d >= 0) & (z - d != r))
             def _():
                 to_right(z - d, q).wait_recv()
 
@@ -175,7 +231,7 @@
 
                 process(z - d, q)
 
-            @pl.when(z + d < nz)
+            @pl.when((z + d < nz) & (z + d != r))
             def _():
                 to_left(z + d, q).wait_recv()
 
@@ -185,11 +241,37 @@
 
                 process(z + d, q)
 
+            @pl.when((d == 1) & (q == n // 2) & (r != z))
+            def _():
+                copy(pz.at[r], pz.at[r], fwd_sem.at[r], pz_sem.at[r], dev(z, z)).wait_recv()
+                spread_all(lambda d: d.start())
+
         add_step(d - 1)
+        pass_step(d - 2)
+
+    trans = (((1,), (1,)), ((), ()))
+
+    @pl.loop(0, n)
+    def _(q):
+        @pl.when(z == r)
+        def _():
+            ext[q] = jnp.zeros(ext.shape[1:], f32)
+
+        @pl.when(z != r)
+        def _():
+            @pl.when(q != r)
+            def _():
+                copy(pz.at[q], pz.at[q], fwd_sem.at[q], pz_sem.at[q], dev(q, z)).wait_recv()
+
+            x = pz[q]
+            total = product(x[:, :cols], a_hi[0], a_lo[0], trans)
+            for h in range(1, g):
+                total = total + product(x[:, h * cols : (h + 1) * cols], a_hi[h], a_lo[h], trans)
+            ext[q] = total
 
     add_step(nz - 1)
-
-    trans = (((1,), (1,)), ((), ()))
+    pass_step(nz - 2)
+    pass_step(nz - 1)
 
     def dpart_copy(q):
         return copy(dpart.at[q], drecv.at[r], dp_sem.at[q], dr_sem.at[r], dev(q, z))
@@ -200,7 +282,7 @@
         def _():
             copy(sums.at[0], fin.at[q], sum_sem.at[0], fin_sem.at[q], dev(q, r)).wait_recv()
 
-        x = -fin[q]
+        x = -(fin[q] + ext[q])
         inv_ref[pl.ds(pl.multiple_of(q * ch, ch), ch), :] = x
         dpart[q] = product(x, m_hi[...], m_lo[...], trans)
 
@@ -234,21 +316,25 @@
     def _(b):
         @pl.loop(0, n)
         def _(q):
-            @pl.when((z < nz - 1) & (b <= z))
+            @pl.when((z < nz - 1) & (b <= z) & (b != r))
             def _():
                 to_right(b, q).wait_send()
 
-            @pl.when((z > 0) & (b >= z))
+            @pl.when((z > 0) & (b >= z) & (b != r))
             def _():
                 to_left(b, q).wait_send()
 
-            @pl.when(q != r)
+            @pl.when((q != r) & ((b != r) | (b == z)))
             def _():
                 part_copy(b, q).wait_send()
 
         @pl.when(jnp.logical_not((z == r) & (b == z)))
         def _():
             sum_copy(b).wait_send()
+
+        @pl.when((z == r) & (b != z))
+        def _():
+            detour_out(b).wait_send()
 
     @pl.loop(0, n)
     def _(q):
@@ -256,6 +342,11 @@
         def _():
             dpart_copy(q).wait_send()
 
+        @pl.when((z == r) & (q != z))
+        def _():
+            scatter(q).wait_send()
+
+    spread_all(lambda d: d.wait_send())
     for o in range(1, n):
         out_copy(o).wait_send()
     for o in range(1, n):
@@ -295,10 +386,14 @@
             pltpu.VMEM((n, ch, width), f32),
             pltpu.VMEM((ch, width), f32),
             pltpu.VMEM((n, ch, width), f32),
+            pltpu.VMEM((n, ch, span), f32),
+            pltpu.VMEM((n, ch, span), f32),
+            pltpu.VMEM((nz, ch, span), f32),
             dma((g - 1,)), dma((g - 1,)),
             dma((nz, n)), dma((nz, n)), dma((nz, n)), dma((nz, n)), dma((nz, n)),
             dma((nz,)), dma((n,)),
             dma((n,)), dma((n,)), dma((n - 1,)), dma((n,)),
+            dma((n,)), dma((n,)), dma((n,)), dma((nz,)), dma((nz,)),
         ],
         compiler_params=pltpu.CompilerParams(
             collective_id=0, has_side_effects=True, vmem_limit_bytes=60 * 1024 * 1024

time: 127 us -> 123 us (0.969)
  the two profiles are of different devices: /device:TPU:24 before, /device:TPU:0 now
where the time goes in v2:
time: 123 us
  Pallas kernels  119 us (97%)
  local copies, waits for them, and re-layouts  3.06 us (2%)
    pallas_call x1, Pallas kernels, local(): pl.pallas_call(functools.partial(kernel, n, nz, g), out_shape=(jax.ShapeD...  119 us
    unnamed x4, local copies, waits for them, and re-layouts  3.06 us

profile of v2, /device:TPU:0, one launch (start us, length us, event | category | flops | bytes accessed | tf_op | source)
XLA Modules:
  0.0 122.8 jit_solution(6329731391760070405)
XLA Ops:
  0.6 119.1 %shard_map.59 = (f32[256,1024]{1,0:T(8,128)}, f32[1,256,256]{2,1,0:T(8,128)}) custom-call(s32[8,16]{1,0:T(8,128)} %st_ref.1, f32[1,256,1024]{2,1,0:T(8,128)} %panel_ref.1, f32[1024,512]{1,0:T(8,128)} %anc_ref.1, f32[1,256,256]{2,1,0:T(8,128)} %diag_ref.1), custom_call_target="tpu_custom_call" | custom-call | tf_op jit(solution)/shard_map/pallas_call | solution.py:366
  119.7 0.0 copy-start
  119.8 2.3 %copy.8 = f32[256,1024]{1,0:T(8,128)} copy(f32[256,1024]{1,0:T(8,128)} %get-tuple-element.4) | data formatting | bytes 2097152
  122.1 0.0 copy-done
  122.1 0.7 copy.9
Async XLA Ops:
  119.7 2.4 %copy-start = (f32[1,256,256]{2,1,0:T(8,128)S(1)}, f32[1,256,256]{2,1,0:T(8,128)}, u32[]{:S(2)}) copy-start(f32[1,256,256]{2,1,0:T(8,128)} %get-tuple-element.5) | copy-start | bytes 786436

commit v3 on v2

--- a/solution.py
+++ b/solution.py
@@ -32,10 +32,10 @@
     n, nz, g,
     st_ref, panel_ref, anc_ref, diag_ref, inv_ref, out_diag_ref,
     gath, part, rs, sums, fin, a_recv, a_hi, a_lo, m_hi, m_lo, dpart, drecv, dsum, dout,
-    pz, ext, rel,
+    pz, ext,
     a_send_sem, a_recv_sem, right_sem, left_sem, gath_sem, part_sem, rs_sem,
     sum_sem, fin_sem, dp_sem, dr_sem, db_sem, do_sem,
-    scat_sem, fwd_sem, pz_sem, rel_sem, out_sem,
+    scat_sem, fwd_sem, pz_sem,
 ):
     r = lax.axis_index("prow")
     me = lax.axis_index("pcol")
@@ -91,12 +91,6 @@
     def sum_copy(b):
         return copy(sums.at[b], fin.at[r], sum_sem.at[b], fin_sem.at[r], dev(z, b))
 
-    def detour(b):
-        return copy(sums.at[b], rel.at[b], sum_sem.at[b], rel_sem.at[b], dev(z, z))
-
-    def detour_out(b):
-        return copy(rel.at[b], fin.at[b], out_sem.at[b], fin_sem.at[b], dev(z, b))
-
     def scatter(q):
         return copy(gath.at[z, q], pz.at[q], scat_sem.at[q], pz_sem.at[q], dev(q, z))
 
@@ -117,15 +111,6 @@
         @pl.when((z > 0) & (z != r))
         def _():
             to_left(z, q).start()
-
-        @pl.when((z == r) & (z != q))
-        def _():
-            scatter(q).start()
-
-    @pl.when(z == r)
-    def _():
-        pz[r] = gath[z, r]
-        spread_all(lambda d: d.start())
 
     @pl.loop(0, nz)
     def _(b):
@@ -183,22 +168,24 @@
         def _():
             fin[r] = sums[b]
 
-        @pl.when((b != z) & (b == r))
-        def _():
-            detour(b).start()
-
-        @pl.when(jnp.logical_not(home) & ((b == z) | (b != r)))
+        @pl.when(jnp.logical_not(home))
         def _():
             sum_copy(b).start()
-
-    def pass_on(b):
-        detour(b).wait_recv()
-        detour_out(b).start()
 
     @pl.loop(0, n)
     def _(q):
         process(z, q)
 
+    @pl.when(z == r)
+    def _():
+        for q in range(n):
+            @pl.when(z != q)
+            def _():
+                scatter(q).start()
+
+        pz[r] = gath[z, r]
+        spread_all(lambda d: d.start())
+
     def add_step(d):
         @pl.when(z - d >= 0)
         def _():
@@ -207,15 +194,6 @@
         @pl.when((z + d < nz) & (d > 0))
         def _():
             add_up(z + d)
-
-    def pass_step(d):
-        @pl.when((z == r) & (z - d >= 0) & (d > 0))
-        def _():
-            pass_on(z - d)
-
-        @pl.when((z == r) & (z + d < nz) & (d > 0))
-        def _():
-            pass_on(z + d)
 
     @pl.loop(1, nz)
     def _(d):
@@ -241,13 +219,12 @@
 
                 process(z + d, q)
 
-            @pl.when((d == 1) & (q == n // 2) & (r != z))
+            @pl.when((d == min(2, nz - 1)) & (q == 0) & (r != z))
             def _():
                 copy(pz.at[r], pz.at[r], fwd_sem.at[r], pz_sem.at[r], dev(z, z)).wait_recv()
                 spread_all(lambda d: d.start())
 
         add_step(d - 1)
-        pass_step(d - 2)
 
     trans = (((1,), (1,)), ((), ()))
 
@@ -270,8 +247,6 @@
             ext[q] = total
 
     add_step(nz - 1)
-    pass_step(nz - 2)
-    pass_step(nz - 1)
 
     def dpart_copy(q):
         return copy(dpart.at[q], drecv.at[r], dp_sem.at[q], dr_sem.at[r], dev(q, z))
@@ -331,10 +306,6 @@
         @pl.when(jnp.logical_not((z == r) & (b == z)))
         def _():
             sum_copy(b).wait_send()
-
-        @pl.when((z == r) & (b != z))
-        def _():
-            detour_out(b).wait_send()
 
     @pl.loop(0, n)
     def _(q):
@@ -388,12 +359,11 @@
             pltpu.VMEM((n, ch, width), f32),
             pltpu.VMEM((n, ch, span), f32),
             pltpu.VMEM((n, ch, span), f32),
-            pltpu.VMEM((nz, ch, span), f32),
             dma((g - 1,)), dma((g - 1,)),
             dma((nz, n)), dma((nz, n)), dma((nz, n)), dma((nz, n)), dma((nz, n)),
             dma((nz,)), dma((n,)),
             dma((n,)), dma((n,)), dma((n - 1,)), dma((n,)),
-            dma((n,)), dma((n,)), dma((n,)), dma((nz,)), dma((nz,)),
+            dma((n,)), dma((n,)), dma((n,)),
         ],
         compiler_params=pltpu.CompilerParams(
             collective_id=0, has_side_effects=True, vmem_limit_bytes=60 * 1024 * 1024

time: 123 us -> 118 us (0.959)
  the two profiles are of different devices: /device:TPU:0 before, /device:TPU:24 now
where the time goes in v3:
time: 118 us
  Pallas kernels  114 us (97%)
  local copies, waits for them, and re-layouts  3.06 us (3%)
    pallas_call x1, Pallas kernels, local(): pl.pallas_call(functools.partial(kernel, n, nz, g), out_shape=(jax.ShapeD...  114 us
    unnamed x4, local copies, waits for them, and re-layouts  3.06 us

profile of v3, /device:TPU:24, one launch (start us, length us, event | category | flops | bytes accessed | tf_op | source)
XLA Modules:
  0.0 118.0 jit_solution(7932767607245166135)
XLA Ops:
  0.6 114.3 %shard_map.59 = (f32[256,1024]{1,0:T(8,128)}, f32[1,256,256]{2,1,0:T(8,128)}) custom-call(s32[8,16]{1,0:T(8,128)} %st_ref.1, f32[1,256,1024]{2,1,0:T(8,128)} %panel_ref.1, f32[1024,512]{1,0:T(8,128)} %anc_ref.1, f32[1,256,256]{2,1,0:T(8,128)} %diag_ref.1), custom_call_target="tpu_custom_call" | custom-call | tf_op jit(solution)/shard_map/pallas_call | solution.py:337
  115.0 0.0 copy-start
  115.0 2.3 %copy.8 = f32[256,1024]{1,0:T(8,128)} copy(f32[256,1024]{1,0:T(8,128)} %get-tuple-element.4) | data formatting | bytes 2097152
  117.3 0.0 copy-done
  117.3 0.7 copy.9
Async XLA Ops:
  115.0 2.4 %copy-start = (f32[1,256,256]{2,1,0:T(8,128)S(1)}, f32[1,256,256]{2,1,0:T(8,128)}, u32[]{:S(2)}) copy-start(f32[1,256,256]{2,1,0:T(8,128)} %get-tuple-element.5) | copy-start | bytes 786436
